TPU v7x, 32 devices: a whole 2x2x4 slice. The times are simulated.
32 devices in a mesh: stn: 4 (over z), tm: 8 (over y, x, core).
Axes of the slice: x: 2, y: 2, z: 4, core: 2. Of those that a mesh axis runs over, the one named last changes fastest.
Arguments:
- voltages: bfloat16 [128, 2, 2, 256, 2048], P('tm', None, None, 'stn'), may hold values from -6 to 6
- taps: float32 [16, 2048], replicated, may hold values from -1.5 to 1.5
- sk_tolerance: float32 [384], P('tm'), may hold values from 0.05 to 0.3
- station_coords: int32 [256, 2], replicated, may hold values from 0 to 1023
- pointings: int32 [256, 2], replicated, may hold values from -64 to 64
- station_flags: int32 [256], replicated, may hold values 0 or 1
Outputs:
- beam_power: float32 [384, 8, 256], P('tm', None, 'stn')
All inputs are finite; a program needn't handle non-finite values.
Results may differ from a plain program's by a relative error of at most 0.0045.
Values may be sent and summed in bfloat16 or wider, within the bound.
A program may use at most 128 MiB of HBM per device.

v0:
```python
import functools
import math

import jax
import jax.numpy as jnp
from jax import lax
from jax.experimental import pallas as pl
from jax.experimental.pallas import tpu as pltpu
from jax.sharding import PartitionSpec as P

INTEG = 16
FINE = 16
LANES = 128
LIMIT = 60 * 1024 * 1024


def divides_evenly(v_count, h_count):
    return v_count == h_count and v_count > 4 and v_count % 2 == 0


def tap_sums(rows, count):
    if not divides_evenly(count, len(rows)):
        return list(rows)
    half = count // 2
    low, high = rows[:half], rows[half:]
    both = [a + b for a, b in zip(low, high)]
    return tap_sums(low, half) + tap_sums(high, half) + tap_sums(both, half)


def convolve(values, gains, at=0):
    count = len(values)
    if count <= 4 or count % 2:
        out = [None] * (2 * count - 1)
        rows = [gains(at + k) for k in range(count)]
        for f in range(count):
            for k in range(count):
                term = values[f] * rows[k]
                out[f + k] = term if out[f + k] is None else out[f + k] + term
        return out, at + count
    half = count // 2
    low, high = values[:half], values[half:]
    sums = [a + b for a, b in zip(low, high)]
    rows = at
    step = sum_rows(half)
    last, _ = convolve(high, gains, rows + step)
    first, _ = convolve(low, gains, rows)
    bias = []
    for i in range(2 * half - 1):
        both = first[i] + last[i]
        spot = half + i
        if spot < 2 * half - 1:
            both = first[spot] - both
        elif spot >= 2 * half:
            both = last[spot - 2 * half] - both
        else:
            both = -both
        bias.append(both)
    middle, _ = convolve(sums, gains, rows + 2 * step)
    middle = [m + b for m, b in zip(middle, bias)]
    return first[:half] + middle + last[half - 1 :], rows + 3 * step


def sum_rows(count):
    return count if count <= 4 or count % 2 else 3 * sum_rows(count // 2)


def turning_points(channels, points):
    columns = jnp.arange(points, dtype=jnp.int32)

    def pair(rows):
        residue = rows[:, None] * columns[None, :] % points
        angle = 2.0 * math.pi / points * residue.astype(jnp.float32)
        return jnp.cos(angle), jnp.sin(angle)

    factor = 1.0 / math.sqrt(points)
    coarse = [x * factor for x in pair(jnp.arange(channels // FINE, dtype=jnp.int32) * FINE)]
    return *coarse, *pair(jnp.arange(FINE, dtype=jnp.int32))


def lane_order(x, local):
    share = LANES // local
    sets = x.shape[0] // (share * local)
    split = x.reshape(sets, share // 2, 2, local // 8, 8, *x.shape[1:])
    return jnp.swapaxes(split, 2, 3).reshape(x.shape)


def steering(first, coords, flags, pointings, scale, local):
    coords, flags = lane_order(coords, local), lane_order(flags, local)
    offsets = coords[:, 0:1] * pointings[None, :, 0] + coords[:, 1:2] * pointings[None, :, 1]
    gain = ((1 - flags).astype(jnp.float32) * scale)[:, None]

    def turn(residue):
        angle = 2.0 * math.pi / 65536.0 * (residue % 65536).astype(jnp.float32)
        return jnp.cos(angle), jnp.sin(angle)

    pr, pi = turn((first + 1) * offsets)
    rr, ri = turn(offsets)
    return pr * gain, pi * gain, rr, ri


def beam_powers(tile, tolerance, weight, left_ref, blocks, groups, local):
    rows = left_ref.shape[1] // blocks
    tiles = rows // 2
    turned = lax.broadcasted_iota(jnp.int32, (rows, 1), 0) < tiles
    beams = weight.shape[1] // 2
    share = LANES // local
    frames = tiles * share
    windows = 2
    half = blocks // windows
    size = float(half * frames)

    lane = lax.broadcasted_iota(jnp.int32, (1, LANES), 1)
    kind = lane // (2 * local) * 2 + lane // 8 % 2

    def moved(x, source, target):
        pairs = target // 2 - source // 2
        shift = (pairs * 2 * local + (target % 2 - source % 2) * 8) % LANES
        return pltpu.roll(x, shift, 1) if shift else x

    def chosen(pieces):
        out = pieces[0]
        for q in range(1, share):
            out = jnp.where(kind == q, pieces[q], out)
        return out

    def folded(x):
        totals = []
        for q in range(share):
            total = x
            for k in range(share):
                if k != q:
                    total = total + moved(x, k, q)
            totals.append(total)
        return chosen(totals)

    first, second = [], []
    for w in range(windows):
        for g in range(groups):
            s1 = jnp.zeros((rows, LANES), jnp.float32)
            s2 = jnp.zeros((rows, LANES), jnp.float32)
            for b in range(w * half, (w + 1) * half):
                v = tile(b, g)
                power = v * v
                power = power + pltpu.roll(power, tiles, 0)
                s1 = s1 + power
                s2 = s2 + power * power
            first.append(jnp.sum(s1, 0, keepdims=True) * 0.5)
            second.append(jnp.sum(s2, 0, keepdims=True) * 0.5)
    first = folded(jnp.concatenate(first, 0))
    second = folded(jnp.concatenate(second, 0))
    kurtosis = (size + 1.0) / (size - 1.0) * (size * second / (first * first) - 1.0)
    deviation = (kurtosis - 1.0) / tolerance
    soft = 1.0 / (1.0 + deviation * deviation)
    for b in range(blocks):
        w = b // half
        pieces = [tile(b, g) * soft[w * groups + g : w * groups + g + 1] for g in range(groups)]
        for k in range(share):
            for at in range(0, groups, share):
                mixed = chosen([moved(pieces[at + q], k, q) for q in range(share)])
                column = at * local
                left_ref[k, b * rows : (b + 1) * rows, column : column + LANES] = mixed.astype(jnp.bfloat16)
    result = [None] * blocks
    for k in range(share):
        beam = jnp.dot(left_ref[k], weight, preferred_element_type=jnp.float32)
        for b in range(blocks):
            block = beam[b * rows : (b + 1) * rows]
            crossed = pltpu.roll(block[:, beams:], tiles, 0)
            value = block[:, :beams] + jnp.where(turned, -crossed, crossed)
            squares = value * value
            result[b] = squares if result[b] is None else result[b] + squares
    return jnp.concatenate([jnp.sum(r, 0, keepdims=True) for r in result], 0)


def whole_kernel(
    blocks, groups, owned, local, polars,
    tol_ref, pr_ref, pi_ref, rr_ref, ri_ref, taps_ref, cc_ref, cs_ref, fc_ref, fs_ref, volt_ref, out_ref,
    volt, sums, table, x_ref, own, acc, carried, came, spread, outgoing, arrived, weights, left, real, imag,
    power, beams_out, beams_in,
    volt_sem, carry_send, carry_recv, send_sem, recv_sem, beam_send, beam_recv,
):
    units, _, count, rows, _ = arrived.shape
    _, frames, parts, sub, chunk = volt.shape
    chunks, outs, _ = table.shape
    tiles = own.shape[1]
    channels = outs // 2
    halves = units // polars
    slots = groups * count
    devices = blocks * groups
    beams = pr_ref.shape[1]
    row_blocks = sub // 8
    lane_blocks = chunk // LANES
    share = max(8, row_blocks)
    pieces = parts * lane_blocks * row_blocks // share
    tm, stn = lax.axis_index("tm"), lax.axis_index("stn")
    me = tm * groups + stn

    def loop(start, stop, body):
        lax.fori_loop(start, stop, lambda k, unused: (body(k), unused)[1], 0)

    def load(n):
        u, i = n // chunks, lax.rem(n, chunks)
        station = pl.multiple_of(lax.rem(u, halves) * sub, sub)
        sample = pl.multiple_of(i * chunk, chunk)
        return pltpu.make_async_copy(
            volt_ref.at[:, :, u // halves, pl.ds(station, sub), pl.ds(sample, chunk)],
            volt.at[lax.rem(n, 2)],
            volt_sem.at[lax.rem(n, 2)],
        )

    def carry(u):
        return pltpu.make_async_remote_copy(
            src_ref=carried.at[u],
            dst_ref=came.at[u],
            send_sem=carry_send.at[u],
            recv_sem=carry_recv.at[u],
            device_id={"tm": lax.rem(tm + 1, blocks), "stn": stn},
            device_id_type=pl.DeviceIdType.MESH,
        )

    def parcel(u, k, arriving):
        to = lax.rem(me + k, devices)
        spot = lax.rem(me + devices - k, devices) if arriving else me
        return pltpu.make_async_remote_copy(
            src_ref=outgoing.at[u, pl.ds(to * count, count)],
            dst_ref=arrived.at[u, spot],
            send_sem=send_sem.at[u, k],
            recv_sem=recv_sem.at[u, spot],
            device_id={"tm": to // groups, "stn": lax.rem(to, groups)},
            device_id_type=pl.DeviceIdType.MESH,
        )

    def tabulated(i):
        at = pl.ds(pl.multiple_of(i * chunk, chunk), chunk)

        def step(n):
            a, b = cc_ref[pl.ds(n, 1), at], cs_ref[pl.ds(n, 1), at]
            c, d = fc_ref[:, at], fs_ref[:, at]
            cosine = a * c - b * d
            sine = b * c + a * d
            over = pl.ds(pl.multiple_of(n * FINE, FINE), FINE)
            under = pl.ds(pl.multiple_of(channels + n * FINE, FINE), FINE)
            table[i, over, :chunk] = cosine.astype(jnp.bfloat16)
            table[i, over, chunk:] = sine.astype(jnp.bfloat16)
            table[i, under, :chunk] = (-sine).astype(jnp.bfloat16)
            table[i, under, chunk:] = cosine.astype(jnp.bfloat16)

        loop(0, channels // FINE, step)

    def filtered(slot, i, j):
        for t in range(share):
            eight = t % row_blocks
            rest = j * (share // row_blocks) + t // row_blocks
            part = rest // lane_blocks
            shift = rest % lane_blocks * LANES
            lane = pl.multiple_of(shift, LANES)
            sample = pl.multiple_of(i * chunk + shift, LANES)
            column = pl.multiple_of(part * chunk + shift, LANES)
            row, low = eight // 2 * 16, eight % 2 * 8
            values = [
                volt[slot, f, part, row : row + 16, pl.ds(lane, LANES)].astype(jnp.float32)[low : low + 8]
                for f in range(frames)
            ]
            out, _ = convolve(values, lambda k: sums[k : k + 1, pl.ds(sample, LANES)])
            out.append(jnp.zeros((8, LANES), jnp.float32))
            for f in range(0, 2 * frames, 2):
                at = (f // 2 * row_blocks + eight) * 16
                pair = jnp.concatenate([out[f], out[f + 1]], 0).astype(jnp.bfloat16)
                x_ref[at : at + 16, pl.ds(column, LANES)] = pair

    def multiplied(u, i):
        product = lax.dot_general(
            table[i], x_ref[...], (((1,), (1,)), ((), ())), preferred_element_type=jnp.float32
        )
        for t in range(tiles):
            own[u % 2, t] = own[u % 2, t] + product[:, t * LANES : (t + 1) * LANES]
            acc[t] = acc[t] + product[:, (tiles + t) * LANES : (tiles + t + 1) * LANES]

    block = math.lcm(owned, 16)
    pitch = block + 8

    def combined(u):
        def step(i):
            for part in range(2):
                for t in range(tiles):
                    at = pl.ds(pl.multiple_of(part * channels + i * block, 16), block)
                    total = own[u % 2, t, at, :] + came[u, t, at, :].astype(jnp.float32)
                    base = (part * tiles + t) * pitch
                    spread[base : base + block, :] = total
            for c in range(block):
                values = spread[pl.ds(c, rows, pitch), :].astype(jnp.bfloat16)
                slot = c // owned * slots + c % owned
                outgoing[u, i * (block // owned) * slots + slot] = values

        loop(0, channels // block, step)

    def finished(u):
        @pl.when(tm > 0)
        def _():
            carry(u).wait_recv()

        combined(u)
        loop(1, devices, lambda k: parcel(u, k, False).start())
        arrived[u, me] = outgoing[u, pl.ds(me * count, count)]

    load(0).start()
    prepared = tap_sums([taps_ref[k : k + 1, :] for k in range(frames)], frames)
    for k, row in enumerate(prepared):
        sums[k : k + 1, :] = row

    @pl.when(tm == 0)
    def _():
        came[...] = jnp.zeros_like(came)

    if slots > owned:
        outgoing[...] = jnp.zeros_like(outgoing)

    def unit(u):
        own[u % 2] = jnp.zeros(own.shape[1:], jnp.float32)
        acc[...] = jnp.zeros_like(acc)

        def step(i):
            n = u * chunks + i
            load(n).wait()

            @pl.when(n + 1 < units * chunks)
            def _():
                load(n + 1).start()

            @pl.when(u == 0)
            def _():
                tabulated(i)

            loop(0, pieces, lambda j: filtered(lax.rem(n, 2), i, j))
            multiplied(u, i)

        loop(0, chunks, step)
        for t in range(tiles):
            carried[u, t] = acc[t].astype(jnp.bfloat16)

        @pl.when(u > 0)
        def _():
            finished(u - 1)

        @pl.when(tm < blocks - 1)
        def _():
            carry(u).start()

    loop(0, units, unit)

    real[...] = pr_ref[...]
    imag[...] = pi_ref[...]

    def turn(c):
        a, b, e, d = real[...], imag[...], rr_ref[...], ri_ref[...]
        weights[c, :, :beams] = a.astype(jnp.bfloat16)
        weights[c, :, beams:] = b.astype(jnp.bfloat16)
        real[...] = a * e - b * d
        imag[...] = a * d + b * e

    loop(0, count, turn)
    finished(units - 1)
    together = 2 if count % 2 == 0 else 1
    depth = left.shape[0] // 2

    def beamed(p):
        for h in range(halves):
            loop(1, devices, lambda k: parcel(p * halves + h, k, True).wait_recv())

        def step(n):
            for o in range(together):
                c = n * together + o

                def tile(b, g):
                    source = arrived[p * halves + g % halves, b * groups + g // halves, c]
                    return source.astype(jnp.float32)

                tolerance = jnp.full((1, LANES), tol_ref[c], jnp.float32)
                result = beam_powers(
                    tile, tolerance, weights[c], left.at[pl.ds(o * depth, depth)], blocks, groups * halves, sub
                )
                power[c] = result if p == 0 else power[c] + result

        loop(0, count // together, step)

    for p in range(polars):
        beamed(p)
    wide = beams // groups
    for c in range(count):
        total = power[c] * (1.0 / (2.0 * INTEG))
        for g in range(groups):
            beams_out[g, c] = total[:, g * wide : (g + 1) * wide]

    def portion(k, arriving):
        to = lax.rem(stn + k, groups)
        spot = lax.rem(stn + groups - k, groups) if arriving else stn
        return pltpu.make_async_remote_copy(
            src_ref=beams_out.at[to],
            dst_ref=beams_in.at[spot],
            send_sem=beam_send.at[k],
            recv_sem=beam_recv.at[spot],
            device_id={"tm": tm, "stn": to},
            device_id_type=pl.DeviceIdType.MESH,
        )

    for k in range(1, groups):
        portion(k, False).start()
    beams_in[stn] = beams_out[stn]

    @pl.when(tm < blocks - 1)
    def _():
        loop(0, units, lambda u: carry(u).wait_send())

    loop(0, units, lambda u: loop(1, devices, lambda k: parcel(u, k, False).wait_send()))
    for k in range(1, groups):
        portion(k, True).wait_recv()
    for i in range(owned):
        out_ref[i] = beams_in[i // count, i % count]
    for k in range(1, groups):
        portion(k, False).wait_send()


def whole_program(voltages, taps, turns, bases, tolerance, owned, blocks, groups, sub):
    frames, parts, polars, local, points = voltages.shape
    channels = owned * blocks
    chunk = min(512, points)
    chunks = points // chunk
    stations, beams = bases[0].shape
    count = tolerance.shape[0]
    tiles = frames * sub // LANES
    rows = 2 * tiles
    units = polars * (local // sub)
    devices = blocks * groups
    wide = beams // groups
    block = math.lcm(owned, 16)
    prepared = 3 ** max(0, int(math.log2(frames)) - 2) * min(frames, 4)
    vmem = pl.BlockSpec(memory_space=pltpu.VMEM)
    flops = 8 * units * frames * sub * channels * parts * points
    return pl.pallas_call(
        functools.partial(whole_kernel, blocks, groups, owned, local, polars),
        in_specs=[pl.BlockSpec(memory_space=pltpu.SMEM)] + [vmem] * 9 + [pl.BlockSpec(memory_space=pl.ANY)],
        out_specs=vmem,
        out_shape=jax.ShapeDtypeStruct((owned, blocks, wide), jnp.float32),
        scratch_shapes=[
            pltpu.VMEM((2, frames, parts, sub, chunk), jnp.bfloat16),
            pltpu.VMEM((prepared, points), jnp.float32),
            pltpu.VMEM((chunks, 2 * channels, parts * chunk), jnp.bfloat16),
            pltpu.VMEM((2 * frames * sub, parts * chunk), jnp.bfloat16),
            pltpu.VMEM((2, tiles, 2 * channels, LANES), jnp.float32),
            pltpu.VMEM((tiles, 2 * channels, LANES), jnp.float32),
            pltpu.VMEM((units, tiles, 2 * channels, LANES), jnp.bfloat16),
            pltpu.VMEM((units, tiles, 2 * channels, LANES), jnp.bfloat16),
            pltpu.VMEM((rows * (block + 8), LANES), jnp.float32),
            pltpu.VMEM((units, devices * count, rows, LANES), jnp.bfloat16),
            pltpu.VMEM((units, devices, count, rows, LANES), jnp.bfloat16),
            pltpu.VMEM((count, stations, 2 * beams), jnp.bfloat16),
            pltpu.VMEM((2 * (LANES // sub), blocks * rows, stations), jnp.bfloat16),
            pltpu.VMEM((stations, beams), jnp.float32),
            pltpu.VMEM((stations, beams), jnp.float32),
            pltpu.VMEM((count, blocks, beams), jnp.float32),
            pltpu.VMEM((groups, count, blocks, wide), jnp.float32),
            pltpu.VMEM((groups, count, blocks, wide), jnp.float32),
            pltpu.SemaphoreType.DMA((2,)),
            pltpu.SemaphoreType.DMA((units,)),
            pltpu.SemaphoreType.DMA((units,)),
            pltpu.SemaphoreType.DMA((units, devices)),
            pltpu.SemaphoreType.DMA((units, devices)),
            pltpu.SemaphoreType.DMA((groups,)),
            pltpu.SemaphoreType.DMA((groups,)),
        ],
        compiler_params=pltpu.CompilerParams(has_side_effects=True, vmem_limit_bytes=LIMIT),
        cost_estimate=pl.CostEstimate(flops=flops, bytes_accessed=40000000, transcendentals=0),
        name="station_beams",
    )(tolerance, *bases, taps, *turns, voltages)


def per_device(voltages, taps, sk_tolerance, station_coords, pointings, station_flags):
    frames, parts, polars, local, points = voltages.shape
    blocks = lax.axis_size("tm")
    groups = lax.axis_size("stn")
    owned = sk_tolerance.shape[0]
    channels = owned * blocks
    count = -(-owned // groups)
    spare = count * groups - owned
    sub = math.gcd(local, 32)
    share = LANES // sub
    assert frames == INTEG and taps.shape[0] == frames and channels % FINE == 0
    assert share % 2 == 0 and groups * local % LANES == 0
    scale = 1.0 / math.sqrt(groups * local)
    first = lax.axis_index("stn") * count
    start = lax.axis_index("tm") * owned + first
    turns = turning_points(channels, points)
    bases = steering(start, station_coords, station_flags, pointings, scale, sub)
    if spare:
        sk_tolerance = jnp.pad(sk_tolerance, (0, spare), constant_values=1.0)
    tolerance = lax.dynamic_slice_in_dim(sk_tolerance, first, count, 0)
    return whole_program(voltages, taps, turns, bases, tolerance, owned, blocks, groups, sub)


def solution(mesh):
    in_specs = (P("tm", None, None, "stn", None), P(), P("tm"), P(), P(), P())
    out_specs = P("tm", None, "stn")
    return jax.shard_map(
        per_device, mesh=mesh, in_specs=in_specs, out_specs=out_specs, check_vma=False
    )
```

profile of v0, /device:TPU:0, one launch (start us, length us, event | category | flops | bytes accessed | tf_op | source)
XLA Modules:
  0.0 137.6 jit_solution(14559950027896346051)
XLA Ops:
  0.0 1.3 dynamic_slice.3.tol_ref
  1.3 0.7 convert_multiply_fusion
  2.0 0.8 fusion.23
  2.7 0.1 reshape.32
  2.8 0.1 mul.169
  2.9 0.8 reshape.29
  3.7 0.1 reshape.30
  3.9 1.2 fusion.20
  5.1 1.6 %sine_multiply_fusion.1 = (f32[24,2048]{1,0:T(8,128)}, f32[24,2048]{1,0:T(8,128)}) fusion(s32[24]{0:T(128)S(1)} %iota_multiply_fusion), kind=kLoop, calls=%fused_computation.24 | loop fusion | flops 786432 | bytes 393312 | tf_op jit(solution)/shard_map/mul | solution.py:76
  6.7 3.2 %sine_multiply_fusion = (f32[256,256]{1,0:T(8,128)}, f32[256,256]{1,0:T(8,128)}, f32[256,256]{1,0:T(8,128)}, f32[256,256]{1,0:T(8,128)}) fusion(f32[256]{0:T(256)S(1)} %mul.169, s32[256]{0:T(256)S(1)} %bitcast.15, s32[256]{0:T(256)S(1)} %bitcast.17, s32[256]{0:T(256)S(1)} %bitcast.14, s32[256]{0:T(256)S(1)} %bitcast.16, s32[]{:T(128)S(6)} %add.40), kind=kLoop, calls=%fused_computation.15 | loop fusion | flops 2097152 | bytes 1053700 | tf_op jit(solution)/shard_map/mul | solution.py:98
  9.9 126.1 %station_beams.1 = f32[48,8,64]{2,1,0:T(8,128)} custom-call(f32[12]{0:T(128)} %dynamic_slice.3.tol_ref, f32[256,256]{1,0:T(8,128)} %get-tuple-element.6.pr_ref, f32[256,256]{1,0:T(8,128)} %get-tuple-element.5.pi_ref, f32[256,256]{1,0:T(8,128)} %get-tuple-element.8.rr_ref, f32[256,256]{1,0:T(8,128)} %get-tuple-element.7.ri_ref, f32[16,2048]{1,0:T(8,128)} %taps_ref.1, ...), custom_call_target="tpu_custom_call" | custom-call | flops 25769803776 | bytes 40000000 | tf_op jit(solution)/shard_map/station_beams/pallas_call | solution.py:438
  136.0 1.6 %copy.13 = f32[48,8,64]{2,1,0:T(8,128)} copy(f32[48,8,64]{2,1,0:T(8,128)} %station_beams.1) | data formatting | bytes 196608
  (4 shorter events, 0.0 us)
where the time goes:
time: 138 us
  Pallas kernels  126 us (91%)
  other arithmetic  6.72 us (5%)
  local copies, waits for them, and re-layouts  4.75 us (3%)
    pallas_call x1, Pallas kernels, whole_program(): pl.pallas_call(functools.partial(whole_kernel, blocks, groups, owned, loc...  126 us
    mul x1, other arithmetic, steering(): return (pr * gain, pi * gain, rr, ri)  3.2 us

commit v1 on v0

--- a/solution.py
+++ b/solution.py
@@ -64,38 +64,23 @@
     return count if count <= 4 or count % 2 else 3 * sum_rows(count // 2)
 
 
-def turning_points(channels, points):
-    columns = jnp.arange(points, dtype=jnp.int32)
-
-    def pair(rows):
-        residue = rows[:, None] * columns[None, :] % points
-        angle = 2.0 * math.pi / points * residue.astype(jnp.float32)
-        return jnp.cos(angle), jnp.sin(angle)
-
-    factor = 1.0 / math.sqrt(points)
-    coarse = [x * factor for x in pair(jnp.arange(channels // FINE, dtype=jnp.int32) * FINE)]
-    return *coarse, *pair(jnp.arange(FINE, dtype=jnp.int32))
-
-
-def lane_order(x, local):
-    share = LANES // local
-    sets = x.shape[0] // (share * local)
-    split = x.reshape(sets, share // 2, 2, local // 8, 8, *x.shape[1:])
-    return jnp.swapaxes(split, 2, 3).reshape(x.shape)
-
-
-def steering(first, coords, flags, pointings, scale, local):
-    coords, flags = lane_order(coords, local), lane_order(flags, local)
-    offsets = coords[:, 0:1] * pointings[None, :, 0] + coords[:, 1:2] * pointings[None, :, 1]
-    gain = ((1 - flags).astype(jnp.float32) * scale)[:, None]
-
-    def turn(residue):
-        angle = 2.0 * math.pi / 65536.0 * (residue % 65536).astype(jnp.float32)
-        return jnp.cos(angle), jnp.sin(angle)
-
-    pr, pi = turn((first + 1) * offsets)
-    rr, ri = turn(offsets)
-    return pr * gain, pi * gain, rr, ri
+def turned(residue, bits):
+    quarter = bits - 2
+    turn = (residue + (1 << (quarter - 1))) >> quarter
+    rest = (residue - (turn << quarter)).astype(jnp.float32) * (2.0 * math.pi / 2.0**bits)
+    z = rest * rest
+    sine, cosine = 0.0, 0.0
+    for k in range(9, 0, -2):
+        sine = (1.0 if k % 4 == 1 else -1.0) / math.factorial(k) + z * sine
+    sine = rest * sine
+    for k in range(10, -1, -2):
+        cosine = (1.0 if k % 4 == 0 else -1.0) / math.factorial(k) + z * cosine
+    odd = (turn & 1) == 1
+    real = jnp.where(odd, sine, cosine)
+    imag = jnp.where(odd, cosine, sine)
+    real = jnp.where(((turn + 1) & 2) == 2, -real, real)
+    imag = jnp.where((turn & 2) == 2, -imag, imag)
+    return real, imag
 
 
 def beam_powers(tile, tolerance, weight, left_ref, blocks, groups, local):
@@ -173,20 +158,21 @@
 
 def whole_kernel(
     blocks, groups, owned, local, polars,
-    tol_ref, pr_ref, pi_ref, rr_ref, ri_ref, taps_ref, cc_ref, cs_ref, fc_ref, fs_ref, volt_ref, out_ref,
-    volt, sums, table, x_ref, own, acc, carried, came, spread, outgoing, arrived, weights, left, real, imag,
-    power, beams_out, beams_in,
+    tol_ref, sites_ref, aims_ref, taps_ref, volt_ref, out_ref,
+    volt, sums, coarse, fine, table, x_ref, own, carried, came, spread, outgoing, arrived, weights, left,
+    real, imag, turn_real, turn_imag, power, beams_out, beams_in,
     volt_sem, carry_send, carry_recv, send_sem, recv_sem, beam_send, beam_recv,
 ):
     units, _, count, rows, _ = arrived.shape
     _, frames, parts, sub, chunk = volt.shape
     chunks, outs, _ = table.shape
-    tiles = own.shape[1]
+    tiles = own.shape[0]
     channels = outs // 2
     halves = units // polars
     slots = groups * count
     devices = blocks * groups
-    beams = pr_ref.shape[1]
+    beams = aims_ref.shape[1]
+    bits = (chunks * chunk).bit_length() - 1
     row_blocks = sub // 8
     lane_blocks = chunk // LANES
     share = max(8, row_blocks)
@@ -230,11 +216,20 @@
         )
 
     def tabulated(i):
-        at = pl.ds(pl.multiple_of(i * chunk, chunk), chunk)
+        def points_of(rows, stride):
+            row = lax.broadcasted_iota(jnp.int32, (rows, chunk), 0) * stride
+            column = lax.broadcasted_iota(jnp.int32, (rows, chunk), 1) + i * chunk
+            return turned(row * column & ((1 << bits) - 1), bits)
+
+        factor = 1.0 / math.sqrt(chunks * chunk)
+        for k, values in enumerate(points_of(channels // FINE, FINE)):
+            coarse[k] = values * factor
+        for k, values in enumerate(points_of(FINE, 1)):
+            fine[k] = values
 
         def step(n):
-            a, b = cc_ref[pl.ds(n, 1), at], cs_ref[pl.ds(n, 1), at]
-            c, d = fc_ref[:, at], fs_ref[:, at]
+            a, b = coarse[0, pl.ds(n, 1), :], coarse[1, pl.ds(n, 1), :]
+            c, d = fine[0], fine[1]
             cosine = a * c - b * d
             sine = b * c + a * d
             over = pl.ds(pl.multiple_of(n * FINE, FINE), FINE)
@@ -265,15 +260,17 @@
             for f in range(0, 2 * frames, 2):
                 at = (f // 2 * row_blocks + eight) * 16
                 pair = jnp.concatenate([out[f], out[f + 1]], 0).astype(jnp.bfloat16)
-                x_ref[at : at + 16, pl.ds(column, LANES)] = pair
-
-    def multiplied(u, i):
-        product = lax.dot_general(
-            table[i], x_ref[...], (((1,), (1,)), ((), ())), preferred_element_type=jnp.float32
-        )
-        for t in range(tiles):
-            own[u % 2, t] = own[u % 2, t] + product[:, t * LANES : (t + 1) * LANES]
-            acc[t] = acc[t] + product[:, (tiles + t) * LANES : (tiles + t + 1) * LANES]
+                x_ref[i, at : at + 16, pl.ds(column, LANES)] = pair
+
+    def transformed(half):
+        rows_of = pl.ds(half * frames * sub, frames * sub)
+        product = None
+        for i in range(chunks):
+            piece = lax.dot_general(
+                table[i], x_ref[i, rows_of, :], (((1,), (1,)), ((), ())), preferred_element_type=jnp.float32
+            )
+            product = piece if product is None else product + piece
+        return [product[:, t * LANES : (t + 1) * LANES] for t in range(tiles)]
 
     block = math.lcm(owned, 16)
     pitch = block + 8
@@ -283,7 +280,7 @@
             for part in range(2):
                 for t in range(tiles):
                     at = pl.ds(pl.multiple_of(part * channels + i * block, 16), block)
-                    total = own[u % 2, t, at, :] + came[u, t, at, :].astype(jnp.float32)
+                    total = own[t, at, :] + came[u, t, at, :].astype(jnp.float32)
                     base = (part * tiles + t) * pitch
                     spread[base : base + block, :] = total
             for c in range(block):
@@ -315,9 +312,6 @@
         outgoing[...] = jnp.zeros_like(outgoing)
 
     def unit(u):
-        own[u % 2] = jnp.zeros(own.shape[1:], jnp.float32)
-        acc[...] = jnp.zeros_like(acc)
-
         def step(i):
             n = u * chunks + i
             load(n).wait()
@@ -331,27 +325,45 @@
                 tabulated(i)
 
             loop(0, pieces, lambda j: filtered(lax.rem(n, 2), i, j))
-            multiplied(u, i)
 
         loop(0, chunks, step)
-        for t in range(tiles):
-            carried[u, t] = acc[t].astype(jnp.bfloat16)
 
         @pl.when(u > 0)
         def _():
             finished(u - 1)
 
+        for t, part in enumerate(transformed(1)):
+            carried[u, t] = part.astype(jnp.bfloat16)
+
         @pl.when(tm < blocks - 1)
         def _():
             carry(u).start()
 
+        for t, part in enumerate(transformed(0)):
+            own[t] = part
+
     loop(0, units, unit)
 
-    real[...] = pr_ref[...]
-    imag[...] = pi_ref[...]
+    scale = 1.0 / math.sqrt(groups * local)
+    channel = tm * owned + stn * count + 1
+
+    def steered(n):
+        rest, eight = n // (2 * row_blocks), lax.rem(n, row_blocks)
+        spot = (rest * row_blocks + eight) * 2 + lax.rem(n // row_blocks, 2)
+        source = pl.ds(pl.multiple_of(n * 8, 8), 8)
+        target = pl.ds(pl.multiple_of(spot * 8, 8), 8)
+        site = sites_ref[source, :]
+        offsets = site[:, 0:1] * aims_ref[0:1, :] + site[:, 1:2] * aims_ref[1:2, :]
+        gain = (1 - site[:, 2:3]).astype(jnp.float32) * scale
+        a, b = turned(channel * offsets & 65535, 16)
+        real[target, :] = a * gain
+        imag[target, :] = b * gain
+        turn_real[target, :], turn_imag[target, :] = turned(offsets & 65535, 16)
+
+    loop(0, groups * local // 8, steered)
 
     def turn(c):
-        a, b, e, d = real[...], imag[...], rr_ref[...], ri_ref[...]
+        a, b, e, d = real[...], imag[...], turn_real[...], turn_imag[...]
         weights[c, :, :beams] = a.astype(jnp.bfloat16)
         weights[c, :, beams:] = b.astype(jnp.bfloat16)
         real[...] = a * e - b * d
@@ -374,7 +386,7 @@
                     source = arrived[p * halves + g % halves, b * groups + g // halves, c]
                     return source.astype(jnp.float32)
 
-                tolerance = jnp.full((1, LANES), tol_ref[c], jnp.float32)
+                tolerance = jnp.full((1, LANES), tol_ref[stn * count + c], jnp.float32)
                 result = beam_powers(
                     tile, tolerance, weights[c], left.at[pl.ds(o * depth, depth)], blocks, groups * halves, sub
                 )
@@ -419,13 +431,13 @@
         portion(k, False).wait_send()
 
 
-def whole_program(voltages, taps, turns, bases, tolerance, owned, blocks, groups, sub):
+def whole_program(voltages, taps, sites, aims, tolerance, owned, blocks, groups, sub):
     frames, parts, polars, local, points = voltages.shape
     channels = owned * blocks
     chunk = min(512, points)
     chunks = points // chunk
-    stations, beams = bases[0].shape
-    count = tolerance.shape[0]
+    stations, beams = sites.shape[0], aims.shape[1]
+    count = tolerance.shape[0] // groups
     tiles = frames * sub // LANES
     rows = 2 * tiles
     units = polars * (local // sub)
@@ -437,15 +449,16 @@
     flops = 8 * units * frames * sub * channels * parts * points
     return pl.pallas_call(
         functools.partial(whole_kernel, blocks, groups, owned, local, polars),
-        in_specs=[pl.BlockSpec(memory_space=pltpu.SMEM)] + [vmem] * 9 + [pl.BlockSpec(memory_space=pl.ANY)],
+        in_specs=[pl.BlockSpec(memory_space=pltpu.SMEM)] + [vmem] * 3 + [pl.BlockSpec(memory_space=pl.ANY)],
         out_specs=vmem,
         out_shape=jax.ShapeDtypeStruct((owned, blocks, wide), jnp.float32),
         scratch_shapes=[
             pltpu.VMEM((2, frames, parts, sub, chunk), jnp.bfloat16),
             pltpu.VMEM((prepared, points), jnp.float32),
+            pltpu.VMEM((2, channels // FINE, chunk), jnp.float32),
+            pltpu.VMEM((2, FINE, chunk), jnp.float32),
             pltpu.VMEM((chunks, 2 * channels, parts * chunk), jnp.bfloat16),
-            pltpu.VMEM((2 * frames * sub, parts * chunk), jnp.bfloat16),
-            pltpu.VMEM((2, tiles, 2 * channels, LANES), jnp.float32),
+            pltpu.VMEM((chunks, 2 * frames * sub, parts * chunk), jnp.bfloat16),
             pltpu.VMEM((tiles, 2 * channels, LANES), jnp.float32),
             pltpu.VMEM((units, tiles, 2 * channels, LANES), jnp.bfloat16),
             pltpu.VMEM((units, tiles, 2 * channels, LANES), jnp.bfloat16),
@@ -454,6 +467,8 @@
             pltpu.VMEM((units, devices, count, rows, LANES), jnp.bfloat16),
             pltpu.VMEM((count, stations, 2 * beams), jnp.bfloat16),
             pltpu.VMEM((2 * (LANES // sub), blocks * rows, stations), jnp.bfloat16),
+            pltpu.VMEM((stations, beams), jnp.float32),
+            pltpu.VMEM((stations, beams), jnp.float32),
             pltpu.VMEM((stations, beams), jnp.float32),
             pltpu.VMEM((stations, beams), jnp.float32),
             pltpu.VMEM((count, blocks, beams), jnp.float32),
@@ -470,7 +485,7 @@
         compiler_params=pltpu.CompilerParams(has_side_effects=True, vmem_limit_bytes=LIMIT),
         cost_estimate=pl.CostEstimate(flops=flops, bytes_accessed=40000000, transcendentals=0),
         name="station_beams",
-    )(tolerance, *bases, taps, *turns, voltages)
+    )(tolerance, sites, aims, taps, voltages)
 
 
 def per_device(voltages, taps, sk_tolerance, station_coords, pointings, station_flags):
@@ -485,15 +500,11 @@
     share = LANES // sub
     assert frames == INTEG and taps.shape[0] == frames and channels % FINE == 0
     assert share % 2 == 0 and groups * local % LANES == 0
-    scale = 1.0 / math.sqrt(groups * local)
-    first = lax.axis_index("stn") * count
-    start = lax.axis_index("tm") * owned + first
-    turns = turning_points(channels, points)
-    bases = steering(start, station_coords, station_flags, pointings, scale, sub)
+    assert points & (points - 1) == 0
+    sites = jnp.stack([station_coords[:, 0], station_coords[:, 1], station_flags], 1)
     if spare:
         sk_tolerance = jnp.pad(sk_tolerance, (0, spare), constant_values=1.0)
-    tolerance = lax.dynamic_slice_in_dim(sk_tolerance, first, count, 0)
-    return whole_program(voltages, taps, turns, bases, tolerance, owned, blocks, groups, sub)
+    return whole_program(voltages, taps, sites, pointings.T, sk_tolerance, owned, blocks, groups, sub)
 
 
 def solution(mesh):

time: 138 us -> 121 us (0.88)
  Pallas kernels: 126 us -> 118 us
  other arithmetic: 6.72 us -> 0.71 us
  local copies, waits for them, and re-layouts: 4.75 us -> 2.42 us
    pallas_call x1, Pallas kernels: 126 us -> 118 us  [whole_program(): pl.pallas_call(functools.partial(whole_kernel, blocks, groups, owned, loc...]
    mul x4 -> x0, other arithmetic: 5.49 us -> none  [the longest x1 3.2 us: steering(): return (pr * gain, pi * gain, rr, ri)]
where the time goes in v1:
time: 121 us
  Pallas kernels  118 us (98%)
  local copies, waits for them, and re-layouts  2.42 us (2%)
    pallas_call x1, Pallas kernels, whole_program(): pl.pallas_call(functools.partial(whole_kernel, blocks, groups, owned, loc...  118 us

profile of v1, /device:TPU:0, one launch (start us, length us, event | category | flops | bytes accessed | tf_op | source)
XLA Modules:
  0.0 121.2 jit_solution(5971074204240494190)
XLA Ops:
  0.0 0.7 pad_add_fusion
  0.7 0.8 copy.10.sites_ref
  1.5 118.1 %station_beams.1 = f32[48,8,64]{2,1,0:T(8,128)} custom-call(f32[48]{0:T(128)} %tol_ref.1, s32[256,3]{1,0:T(8,128)} %copy.10.sites_ref, s32[2,256]{1,0:T(2,128)} %bitcast.3, f32[16,2048]{1,0:T(8,128)} %taps_ref.1, bf16[16,2,2,64,2048]{4,3,2,1,0:T(8,128)(2,1)} %volt_ref.1), custom_call_target="tpu_custom_call" | custom-call | flops 25769803776 | bytes 40000000 | tf_op jit(solution)/shard_map/station_beams/pallas_call | solution.py:450
  119.6 1.6 %copy.12 = f32[48,8,64]{2,1,0:T(8,128)} copy(f32[48,8,64]{2,1,0:T(8,128)} %station_beams.1) | data formatting | bytes 196608

commit v2 on v1

--- a/solution.py
+++ b/solution.py
@@ -328,7 +328,7 @@
 
         loop(0, chunks, step)
 
-        @pl.when(u > 0)
+        @pl.when(u == 1)
         def _():
             finished(u - 1)
 
@@ -338,6 +338,10 @@
         @pl.when(tm < blocks - 1)
         def _():
             carry(u).start()
+
+        @pl.when(u > 1)
+        def _():
+            finished(u - 1)
 
         for t, part in enumerate(transformed(0)):
             own[t] = part
@@ -371,8 +375,8 @@
 
     loop(0, count, turn)
     finished(units - 1)
-    together = 2 if count % 2 == 0 else 1
-    depth = left.shape[0] // 2
+    together = math.gcd(count, 4)
+    depth = left.shape[0] // 4
 
     def beamed(p):
         for h in range(halves):
@@ -466,7 +470,7 @@
             pltpu.VMEM((units, devices * count, rows, LANES), jnp.bfloat16),
             pltpu.VMEM((units, devices, count, rows, LANES), jnp.bfloat16),
             pltpu.VMEM((count, stations, 2 * beams), jnp.bfloat16),
-            pltpu.VMEM((2 * (LANES // sub), blocks * rows, stations), jnp.bfloat16),
+            pltpu.VMEM((4 * (LANES // sub), blocks * rows, stations), jnp.bfloat16),
             pltpu.VMEM((stations, beams), jnp.float32),
             pltpu.VMEM((stations, beams), jnp.float32),
             pltpu.VMEM((stations, beams), jnp.float32),

time: 121 us -> 123 us (1.017)
  Pallas kernels: 118 us -> 120 us
    pallas_call x1, Pallas kernels: 118 us -> 120 us  [whole_program(): pl.pallas_call(functools.partial(whole_kernel, blocks, groups, owned, loc...]
where the time goes in v2:
time: 123 us
  Pallas kernels  120 us (98%)
  local copies, waits for them, and re-layouts  2.42 us (2%)
    pallas_call x1, Pallas kernels, whole_program(): pl.pallas_call(functools.partial(whole_kernel, blocks, groups, owned, loc...  120 us

profile of v2, /device:TPU:0, one launch (start us, length us, event | category | flops | bytes accessed | tf_op | source)
XLA Modules:
  0.0 122.6 jit_solution(12452460381241083363)
XLA Ops:
  0.0 0.7 pad_add_fusion
  0.7 0.8 copy.10.sites_ref
  1.5 119.5 %station_beams.1 = f32[48,8,64]{2,1,0:T(8,128)} custom-call(f32[48]{0:T(128)} %tol_ref.1, s32[256,3]{1,0:T(8,128)} %copy.10.sites_ref, s32[2,256]{1,0:T(2,128)} %bitcast.3, f32[16,2048]{1,0:T(8,128)} %taps_ref.1, bf16[16,2,2,64,2048]{4,3,2,1,0:T(8,128)(2,1)} %volt_ref.1), custom_call_target="tpu_custom_call" | custom-call | flops 25769803776 | bytes 40000000 | tf_op jit(solution)/shard_map/station_beams/pallas_call | solution.py:454
  121.0 1.6 %copy.12 = f32[48,8,64]{2,1,0:T(8,128)} copy(f32[48,8,64]{2,1,0:T(8,128)} %station_beams.1) | data formatting | bytes 196608
